TPU v7x, 32 devices: a whole 2x2x4 slice. The times are simulated.
32 devices in a mesh: rows: 16 (over z, y, x), cols: 2 (over core).
Axes of the slice: x: 2, y: 2, z: 4, core: 2. Of those that a mesh axis runs over, the one named last changes fastest.
Arguments:
- embeddings: bfloat16 [49152, 1536], P('rows'), may hold values from -43 to 43, as said below
- start_basis: float32 [1536, 256], P(None, 'cols'), may hold values from -6 to 6
Outputs:
- projected: bfloat16 [49152, 256], P('rows', 'cols')
- basis: float32 [1536, 256], P(None, 'cols')
Inputs may be any that keep to these rules, and one draw needn't show every extreme that they name: `embeddings`: rows are noisy vectors around offsets that differ between aligned blocks of rows, with per-column spreads that differ by a factor of up to four.
All inputs are finite; a program needn't handle non-finite values.
Results may differ from a plain program's by a relative error of at most 0.025.
Values may be sent and summed in bfloat16 or wider, within the bound.
A program may use at most 64 MiB of HBM per device.

v0:
```python
import functools

import jax
import jax.numpy as jnp
from jax import lax
from jax.experimental import pallas as pl
from jax.experimental.pallas import tpu as pltpu
from jax.sharding import PartitionSpec as P

ITERS = 3
PARTS = 3
LANES = 128
MESH = pl.DeviceIdType.MESH
STREAMS = 2 * PARTS
TILES = 4
HI = lax.Precision.HIGHEST
F32 = jnp.float32
BF16 = jnp.bfloat16


def dot(a, b, ca, cb, precision=None):
    return lax.dot_general(a, b, (((ca,), (cb,)), ((), ())), precision=precision, preferred_element_type=F32)


BLOCKS = (((0, 0), (0, 1), (0, 2)), ((1, 1), (1, 2), (2, 2)))


def split(v):
    hi = v.astype(BF16)
    return hi, (v - hi.astype(F32)).astype(BF16)


def pivot_inverse(a):
    m = len(a)
    a = [list(row) for row in a]
    t = [[None] * m for _ in range(m)]
    inv = []
    for j in range(m):
        r = 1.0 / a[j][j]
        inv.append(r)
        for i in range(j + 1, m):
            f = a[i][j] * r
            for c in range(j + 1, i + 1):
                a[i][c] = a[i][c] - f * a[c][j]
            for c in range(j):
                t[i][c] = t[i][c] - f * t[j][c]
            t[i][j] = -f
    return t, inv


def inverse_factor(a_ref, k, b):
    w = 2 * b
    sub = lax.broadcasted_iota(jnp.int32, (8, w), 0)
    eye = (lax.broadcasted_iota(jnp.int32, (b, b), 0) == lax.broadcasted_iota(jnp.int32, (b, b), 1)).astype(F32)
    for blk in range(k // b):
        lo, hi = blk * b, (blk + 1) * b
        aug = jnp.concatenate([a_ref[lo:hi, lo:hi], eye], axis=1)
        tiles = [aug[8 * t:8 * t + 8] for t in range(b // 8)]
        for p in range(b // 8):
            cols = {
                t: [jnp.broadcast_to(tiles[t][:, 8 * p + c:8 * p + c + 1], (8, w)) for c in range(8)]
                for t in range(p, b // 8)
            }
            block = [[jnp.broadcast_to(cols[p][j][i:i + 1], (8, w)) for j in range(i + 1)] for i in range(8)]
            t8, inv = pivot_inverse(block)
            rows = [jnp.broadcast_to(tiles[p][c:c + 1], (8, w)) for c in range(8)]
            low = []
            for i in range(8):
                v = rows[i]
                for c in range(i):
                    v = v + t8[i][c] * rows[c]
                low.append(v)
            scaled = [low[i] * inv[i] for i in range(8)]
            if p + 1 < b // 8:
                solved = []
                for c in range(8):
                    v = scaled[c]
                    for i in range(c + 1, 8):
                        v = v + t8[i][c] * scaled[i]
                    solved.append(v)
                for t in range(p + 1, b // 8):
                    u = [cols[t][c] * solved[c] for c in range(8)]
                    tiles[t] = tiles[t] - (((u[0] + u[1]) + (u[2] + u[3])) + ((u[4] + u[5]) + (u[6] + u[7])))
            v, d = low[0], inv[0]
            for i in range(1, 8):
                v = jnp.where(sub == i, low[i], v)
                d = jnp.where(sub == i, inv[i], d)
            root = lax.rsqrt(d)
            root = root * (1.5 - 0.5 * d * root * root)
            tiles[p] = v * (d * root)
        strip = dot(jnp.concatenate(tiles, axis=0)[:, b:], a_ref[lo:hi, :], 1, 0, HI)
        a_ref[lo:hi, :] = strip
        if hi < k:
            a_ref[hi:, :] -= dot(strip[:, hi:k], strip, 0, 0, HI)


def iterate_kernel(n, total, w_ref, s_ref, b_ref, out_ref, w, basis, mean, mean_t, a):
    d, k = out_ref.shape
    t = d // PARTS
    for c, pairs in enumerate(BLOCKS):
        for slot, (i, j) in enumerate(pairs):
            v = jnp.concatenate([w_ref[c, slot, l] for l in range(t // LANES)], axis=1)
            w[i * t:(i + 1) * t, j * t:(j + 1) * t] = v
            if i != j:
                w[j * t:(j + 1) * t, i * t:(i + 1) * t] = v.T
    s = s_ref[:, 0, :]
    r = s.shape[0]
    m = s * (1.0 / n) - jnp.sum(s, axis=0, keepdims=True) * (1.0 / total)
    mh, ml = split(m)
    mean[:r] = mh
    mean[r:] = ml
    mean_t[...] = jnp.concatenate([mh.astype(F32), ml.astype(F32), mh.astype(F32)], axis=0).T.astype(BF16)
    basis[...] = jnp.concatenate([b_ref[0], b_ref[1]], axis=1)

    @pl.loop(0, ITERS)
    def _(_):
        bf = basis[...]
        inner = dot(mean[...], bf, 1, 0)
        ih, il = split((inner[:r] + inner[r:]) * float(n))
        ph, plo = split(dot(w[...], bf, 1, 0) + dot(mean_t[...], jnp.concatenate([ih, ih, il], axis=0), 1, 0))
        cross = dot(plo, ph, 0, 0)
        a[:, :k] = dot(ph, ph, 0, 0) + (dot(plo, plo, 0, 0) + (cross + cross.T))
        a[:, k:] = (
            lax.broadcasted_iota(jnp.int32, (k, k), 0) == lax.broadcasted_iota(jnp.int32, (k, k), 1)
        ).astype(F32)
        inverse_factor(a, k, 64)
        lh, ll = split(a[:, k:])
        new = dot(ph, lh, 1, 1) + (dot(ph, ll, 1, 1) + dot(plo, lh, 1, 1))
        out_ref[...] = new
        basis[...] = new.astype(BF16)


def iterate(n, total, w, s, b):
    d, k = b.shape[1], 2 * b.shape[2]
    vm = pl.BlockSpec(memory_space=pltpu.VMEM)
    return pl.pallas_call(
        functools.partial(iterate_kernel, n, total),
        in_specs=[vm] * 3,
        out_specs=vm,
        out_shape=jax.ShapeDtypeStruct((d, k), F32),
        scratch_shapes=[
            pltpu.VMEM((d, d), BF16),
            pltpu.VMEM((d, k), BF16),
            pltpu.VMEM((2 * s.shape[0], d), BF16),
            pltpu.VMEM((d, 3 * s.shape[0]), BF16),
            pltpu.VMEM((k, 2 * k), F32),
        ],
    )(w, s, b)


def project_kernel(total, e_ref, s_ref, b_ref, o_ref, basis_ref, mean, bf):
    core = lax.axis_index("cols")
    h = o_ref.shape[1]

    @pl.when(pl.program_id(0) == 0)
    def _():
        mean[...] = jnp.sum(s_ref[:, 0, :], axis=0, keepdims=True) * (1.0 / total)
        full = b_ref[...]
        bf[...] = full.astype(BF16)
        basis_ref[...] = jnp.where(core == 0, full[:, :h], full[:, h:])

    centered = e_ref[...].astype(F32) - mean[...]
    unit = (centered * lax.rsqrt(jnp.sum(centered * centered, axis=1, keepdims=True) + 1.0)).astype(BF16)
    coords = dot(unit, bf[...], 1, 0)
    k = coords.shape[1]
    scale = lax.rsqrt(jnp.sum(coords * coords, axis=1, keepdims=True) * (1.0 / k) + 0.0001)
    o_ref[...] = (jnp.where(core == 0, coords[:, :h], coords[:, h:]) * scale).astype(o_ref.dtype)


def project(total, e, s, b, h, rows=512):
    n, d = e.shape
    k = b.shape[1]
    return pl.pallas_call(
        functools.partial(project_kernel, total),
        grid=(n // rows,),
        in_specs=[
            pl.BlockSpec((rows, d), lambda i: (i, 0)),
            pl.BlockSpec(s.shape, lambda i: (0, 0, 0)),
            pl.BlockSpec((d, k), lambda i: (0, 0)),
        ],
        out_specs=[pl.BlockSpec((rows, h), lambda i: (i, 0)), pl.BlockSpec((d, h), lambda i: (0, 0))],
        out_shape=[jax.ShapeDtypeStruct((n, h), BF16), jax.ShapeDtypeStruct((d, h), F32)],
        scratch_shapes=[pltpu.VMEM((1, d), F32), pltpu.VMEM((d, k), BF16)],
    )(e, s, b)


def factors(r):
    z = 4 if r % 4 == 0 else 1
    x = 1
    while x * x < r // z:
        x *= 2
    return z, r // z // x, x


def reduce_kernel(r, e_hbm, b_ref, wout, sout, bout, e, acc, ssum, w_ref, e_sem, *scratch):
    nz, ny, nx = factors(r)
    plans = (("x", "y", "z"), ("y", "x", "z")) * (STREAMS // 2)
    size = {"x": nx, "y": ny, "z": nz}
    stride = {"x": 1, "y": nx, "z": nx * ny}
    scratch = list(scratch)
    stage = [[scratch.pop(0) for _ in plan] for plan in plans]
    held = [[scratch.pop(0) for _ in plan[:-1]] for plan in plans]
    w_send, w_recv, s_send, s_recv, c_send, c_recv = scratch

    me = lax.axis_index("rows")
    core = lax.axis_index("cols")
    n, d = e.shape
    t = d // PARTS
    tile = n // TILES

    def tile_copy(i):
        at_rows = pl.ds(pl.multiple_of(i * tile, tile), tile)
        return pltpu.make_async_copy(e_hbm.at[at_rows], e.at[at_rows], e_sem.at[i])

    for i in range(TILES):
        tile_copy(i).start()
    at = {a: lax.rem(me // stride[a], size[a]) for a in size}
    partner = {"cols": 1 - core}

    def peer(a, k):
        p = lax.rem(at[a] + k, size[a])
        return p, {"rows": me + (p - at[a]) * stride[a]}

    barrier = pltpu.get_barrier_semaphore()
    count = 1
    pl.semaphore_signal(barrier, inc=1, device_id=partner, device_id_type=MESH)
    for a in size:
        for k in range(1, size[a]):
            pl.semaphore_signal(barrier, inc=1, device_id=peer(a, k)[1], device_id_type=MESH)
            count += 1
    pl.semaphore_wait(barrier, count)

    def remote(src, dst, send, recv, device):
        copy = pltpu.make_async_remote_copy(
            src_ref=src, dst_ref=dst, send_sem=send, recv_sem=recv, device_id=device, device_id_type=MESH
        )
        copy.start()
        return copy

    def rows_of(off, m):
        return pl.ds(pl.multiple_of(off, 16), m)

    length = w_ref.shape[0]
    off = [q * (length // STREAMS) for q in range(STREAMS)]
    span = [length // STREAMS] * STREAMS

    def start_reduce(q, ph):
        a = plans[q][ph]
        g = size[a]
        m = span[q] // g
        copies = []
        for k in range(1, g):
            p, dev = peer(a, k)
            src = w_ref.at[rows_of(off[q] + p * m, m)] if ph == 0 else held[q][ph - 1].at[rows_of(p * m, m)]
            copies.append(
                remote(src, stage[q][ph].at[k - 1], w_send.at[q, ph, k - 1], w_recv.at[q, ph, k - 1], dev)
            )
        return copies

    def finish_reduce(q, ph, copies):
        a = plans[q][ph]
        g = size[a]
        m = span[q] // g
        for c in copies:
            c.wait()
        mine = rows_of(off[q] + at[a] * m, m) if ph == 0 else rows_of(at[a] * m, m)
        total = (w_ref[mine] if ph == 0 else held[q][ph - 1][mine]).astype(F32)
        for k in range(g - 1):
            total = total + stage[q][ph][k].astype(F32)
        off[q] = off[q] + at[a] * m
        span[q] = m
        if ph < len(plans[q]) - 1:
            held[q][ph][...] = total.astype(BF16)
        else:
            wout[core, rows_of(off[q], m)] = total.astype(BF16)

    def start_sums(ph):
        a = "xyz"[ph]
        width = stride[a]
        first = me // width * width
        block = pl.ds(first, width)
        return [
            remote(sout.at[block], sout.at[block], s_send.at[ph, k - 1], s_recv.at[ph, k - 1], peer(a, k)[1])
            for k in range(1, size[a])
        ]

    bout[core] = b_ref[...]
    basis_copy = remote(b_ref, bout.at[core], c_send.at[STREAMS], c_recv.at[STREAMS], partner)
    ssum[...] = jnp.zeros_like(ssum)
    pending = []
    for slot in range(PARTS):
        acc[...] = jnp.zeros_like(acc)
        for c in range(2):
            @pl.when(core == c)
            def _(slot=slot, c=c):
                i, j = BLOCKS[c][slot]

                @pl.loop(0, TILES)
                def _(step):
                    if slot == 0:
                        tile_copy(step).wait()
                    part = pl.ds(pl.multiple_of(step * tile, tile), tile)
                    if slot == 0:
                        ssum[...] += dot(jnp.ones((8, tile), BF16), e[part, :], 1, 0)
                    acc[...] += dot(e[part, i * t:(i + 1) * t], e[part, j * t:(j + 1) * t], 0, 0)

                si = ssum[:, i * t:(i + 1) * t] * (1.0 / (8 * n))
                v = (acc[...] - dot(si, ssum[:, j * t:(j + 1) * t], 0, 0, HI)).astype(BF16)
                for l in range(t // LANES):
                    first = (slot * (t // LANES) + l) * t
                    w_ref[first:first + t, :] = v[:, l * LANES:(l + 1) * LANES]

        if slot == 0:
            sout[me] = ssum[0:1, :]
        pending += [start_reduce(q, 0) for q in (2 * slot, 2 * slot + 1)]
        if slot == 0:
            sums = start_sums(0)
        else:
            for q in (2 * slot - 2, 2 * slot - 1):
                finish_reduce(q, 0, pending[q])
                pending[q] = start_reduce(q, 1)
    for ph in range(3):
        for c in sums:
            c.wait()
        if ph < 2:
            sums = start_sums(ph + 1)
        for q in range(STREAMS):
            if ph == 0 and q < STREAMS - 2:
                continue
            finish_reduce(q, ph, pending[q])
            if ph < 2:
                pending[q] = start_reduce(q, ph + 1)

    def start_gather(q, ph):
        a = plans[q][ph]
        block = wout.at[core, rows_of(off[q], span[q])]
        return [
            remote(block, block, w_send.at[q, 3 + ph, k - 1], w_recv.at[q, 3 + ph, k - 1], peer(a, k)[1])
            for k in range(1, size[a])
        ]

    pending = [start_gather(q, 2) for q in range(STREAMS)]
    across = []
    for ph in (2, 1, 0):
        for q in range(STREAMS):
            a = plans[q][ph]
            for c in pending[q]:
                c.wait()
            off[q] = off[q] - at[a] * span[q]
            span[q] = span[q] * size[a]
            if ph > 0:
                pending[q] = start_gather(q, ph - 1)
            if ph == 1:
                early = rows_of(off[q], span[q])
                block = wout.at[core, early]
                across.append(remote(block, block, c_send.at[q], c_recv.at[q], partner))
            if ph == 0:
                part = span[q] // size[a]
                for k in range(1, size[a]):
                    p = peer(a, k)[0]
                    block = wout.at[core, rows_of(off[q] + p * part, part)]
                    sem = STREAMS + q * (size[a] - 1) + k
                    across.append(remote(block, block, c_send.at[sem], c_recv.at[sem], partner))
    for c in across:
        c.wait()
    basis_copy.wait()


def reduce(r, e, b):
    n, d = e.shape
    t = d // PARTS
    length = PARTS * t * t // LANES
    nz, ny, nx = factors(r)
    stages, helds = [], []
    for sizes in ((nx, ny, nz), (ny, nx, nz)) * (STREAMS // 2):
        m = length // STREAMS
        for ph, g in enumerate(sizes):
            m //= g
            stages.append(pltpu.VMEM((max(g - 1, 1), m, LANES), BF16))
            if ph < 2:
                helds.append(pltpu.VMEM((m, LANES), BF16))
    widest = max(nx, ny, nz) - 1
    sems = ((STREAMS, 6, widest), (3, widest), (1 + STREAMS * (1 + widest),))
    vm = pl.BlockSpec(memory_space=pltpu.VMEM)
    dma = pltpu.SemaphoreType.DMA
    return pl.pallas_call(
        functools.partial(reduce_kernel, r),
        in_specs=[pl.BlockSpec(memory_space=pl.ANY), vm],
        out_specs=[vm] * 3,
        out_shape=[
            jax.ShapeDtypeStruct((2, length, LANES), BF16),
            jax.ShapeDtypeStruct((r, 1, d), F32),
            jax.ShapeDtypeStruct((2,) + b.shape, BF16),
        ],
        scratch_shapes=[
            pltpu.VMEM((n, d), BF16),
            pltpu.VMEM((t, t), F32),
            pltpu.VMEM((8, d), F32),
            pltpu.VMEM((length, LANES), BF16),
            dma((TILES,)),
        ]
        + stages + helds + [dma(shape) for shape in sems for _ in range(2)],
        compiler_params=pltpu.CompilerParams(collective_id=0, has_side_effects=True),
    )(e, b)


def shards(embeddings, start_basis):
    n, d = embeddings.shape
    total = n * lax.axis_size("rows")
    t = d // PARTS
    w, s, b = reduce(lax.axis_size("rows"), embeddings, start_basis.astype(BF16))
    w = w.reshape(2, PARTS, t // LANES, t, LANES)
    basis = iterate(n, total, w, s, b)
    return project(total, embeddings, s, basis, start_basis.shape[1])


def solution(mesh):
    in_specs = (P("rows", None), P(None, "cols"))
    out_specs = (P("rows", "cols"), P(None, "cols"))
    return jax.shard_map(shards, mesh=mesh, in_specs=in_specs, out_specs=out_specs, check_vma=False)
```

profile of v0, /device:TPU:0, one launch (start us, length us, event | category | flops | bytes accessed | tf_op | source)
XLA Modules:
  0.0 127.1 jit_solution(8902952984707282259)
XLA Ops:
  0.6 1.9 %convert_element_type.3.b_ref = bf16[1536,128]{1,0:T(8,128)(2,1)} convert(f32[1536,128]{1,0:T(8,128)} %param.3) | non-fusion elementwise | flops 196608 | bytes 1179648 | tf_op jit(solution)/shard_map/convert_element_type | solution.py:411
  2.5 60.9 %shard_map.41 = (bf16[2,6144,128]{2,1,0:T(8,128)(2,1)}, f32[16,1,1536]{2,1,0:T(1,128)}, bf16[2,1536,128]{2,1,0:T(8,128)(2,1)}) custom-call(bf16[3072,1536]{1,0:T(8,128)(2,1)} %e_ref.1, bf16[1536,128]{1,0:T(8,128)(2,1)} %convert_element_type.3.b_ref), custom_call_target="tpu_custom_call" | custom-call | tf_op jit(solution)/shard_map/pallas_call | solution.py:386
  63.4 53.5 %shard_map.42.b_ref = f32[1536,256]{1,0:T(8,128)} custom-call(bf16[2,3,4,512,128]{4,3,2,1,0:T(8,128)(2,1)} %bitcast.1, f32[16,1,1536]{2,1,0:T(1,128)} %get-tuple-element.5.s_ref, bf16[2,1536,128]{2,1,0:T(8,128)(2,1)} %get-tuple-element.7.b_ref), custom_call_target="tpu_custom_call" | custom-call | tf_op jit(solution)/shard_map/pallas_call | solution.py:136
  117.0 10.1 %shard_map.43 = (bf16[3072,128]{1,0:T(8,128)(2,1)}, f32[1536,128]{1,0:T(8,128)}) custom-call(bf16[3072,1536]{1,0:T(8,128)(2,1)} %e_ref.1, f32[16,1,1536]{2,1,0:T(1,128)} %get-tuple-element.5.s_ref, f32[1536,256]{1,0:T(8,128)} %shard_map.42.b_ref), custom_call_target="tpu_custom_call" | custom-call | tf_op jit(solution)/shard_map/pallas_call | solution.py:173
where the time goes:
time: 127 us
  Pallas kernels  124 us (98%)
  other arithmetic  1.92 us (2%)
    pallas_call x1, Pallas kernels, reduce(): pl.pallas_call(functools.partial(reduce_kernel, r), in_specs=[pl.BlockSpe...  60.9 us
    pallas_call x1, Pallas kernels, iterate(): pl.pallas_call(functools.partial(iterate_kernel, n, total), in_specs=[vm]...  53.5 us
    pallas_call x1, Pallas kernels, project(): pl.pallas_call(functools.partial(project_kernel, total), grid=(n // rows,...  10.1 us

commit v1 on v0

v1 whole, which is shorter than its diff:
```python
import functools

import jax
import jax.numpy as jnp
from jax import lax
from jax.experimental import pallas as pl
from jax.experimental.pallas import tpu as pltpu
from jax.sharding import PartitionSpec as P

ITERS = 3
LANES = 128
MESH = pl.DeviceIdType.MESH
TILES = 4
HI = lax.Precision.HIGHEST
F32 = jnp.float32
BF16 = jnp.bfloat16


def dot(a, b, ca, cb, precision=None):
    return lax.dot_general(a, b, (((ca,), (cb,)), ((), ())), precision=precision, preferred_element_type=F32)


def split(v):
    hi = v.astype(BF16)
    return hi, (v - hi.astype(F32)).astype(BF16)


def inverse_factor(a_ref, spread, k, b):
    w = 2 * b
    lanes = lax.broadcasted_iota(jnp.int32, (b, w), 1)
    subs = lax.broadcasted_iota(jnp.int32, (b, w), 0)
    wide_lane = lax.broadcasted_iota(jnp.int32, (b, k), 1)
    wide_sub = lax.broadcasted_iota(jnp.int32, (b, k), 0)
    sub = lax.broadcasted_iota(jnp.int32, (8, w), 0)
    m = b // 8
    for blk in range(k // b):
        lo, hi = blk * b, (blk + 1) * b
        base = lo % w
        other = b - base
        here = (lanes >= base) & (lanes < base + b)
        first = lo - base
        aug = jnp.where(here, a_ref[lo:hi, first:first + w], (lanes - other == subs).astype(F32))
        tiles = [aug[8 * t:8 * t + 8] for t in range(m)]
        for p in range(m):
            cols = {
                t: [jnp.broadcast_to(tiles[t][:, base + 8 * p + c:base + 8 * p + c + 1], (8, w)) for c in range(8)]
                for t in range(p, m)
            }
            slot = 9 * (p % 2)
            for j in range(8):
                spread[slot + j] = cols[p][j]
            spread[slot + 8] = tiles[p]
            a = [[jnp.broadcast_to(spread[slot + j, i:i + 1, :], (8, w)) for j in range(i + 1)] for i in range(8)]
            low = [jnp.broadcast_to(spread[slot + 8, c:c + 1, :], (8, w)) for c in range(8)]
            inv = []
            for j in range(8):
                r = 1.0 / a[j][j]
                inv.append(r)
                f = {i: a[i][j] * r for i in range(j + 1, 8)}
                for i in range(j + 1, 8):
                    for c in range(j + 1, i + 1):
                        a[i][c] = a[i][c] - f[i] * a[c][j]
                scaled = low[j] * r
                for i in range(j + 1, 8):
                    low[i] = low[i] - f[i] * low[j]
                for t in range(p + 1, m):
                    tiles[t] = tiles[t] - cols[t][j] * scaled
                    for i in range(j + 1, 8):
                        cols[t][i] = cols[t][i] - f[i] * cols[t][j]
            v, d = low[0], inv[0]
            for i in range(1, 8):
                v = jnp.where(sub == i, low[i], v)
                d = jnp.where(sub == i, inv[i], d)
            root = lax.rsqrt(d)
            root = root * (1.5 - 0.5 * d * root * root)
            tiles[p] = v * (d * root)
        factor = jnp.where(here, 0.0, jnp.concatenate(tiles, axis=0))
        inside = (wide_lane >= lo) & (wide_lane < hi)
        rows = jnp.where(inside, (wide_lane - lo == wide_sub).astype(F32), a_ref[lo:hi, :])
        pad = jnp.zeros((b, k), F32)
        strip = dot(factor, jnp.concatenate([pad, rows] if base == 0 else [rows, pad], axis=0), 1, 0, HI)
        for r0 in range(hi, k, b):
            turned = pltpu.roll(a_ref[r0:r0 + b, first:first + w], b, axis=1)
            left = dot(turned, factor, 1, 1, HI)
            old = jnp.where(inside, 0.0, a_ref[r0:r0 + b, :])
            a_ref[r0:r0 + b, :] = old - dot(left, strip, 1, 0, HI)
        a_ref[lo:hi, :] = strip


def finish_kernel(n, total, w_ref, s_ref, b_ref, u_hbm, o_hbm, basis_hbm,
                  w, basis, mean, mean_t, a, spread, unit, out, half, u_sem, o_sem, h_sem):
    core = lax.axis_index("cols")
    d, k = basis.shape
    h = k // 2
    rows = n // TILES

    def unit_copy(i):
        at = pl.ds(pl.multiple_of(i * rows, rows), rows)
        return pltpu.make_async_copy(u_hbm.at[at], unit.at[at], u_sem.at[i])

    for i in range(TILES):
        unit_copy(i).start()
    for (i, l), (c, first, m) in packing(d)[0].items():
        v = w_ref[c, first:first + m, :]
        row, col = i * (d // len(OWNER)), l * LANES
        w[row:row + m, col:col + LANES] = v
        if row + m > col:
            v, m = v[:m - LANES], m - LANES
        if m > 0:
            w[col:col + LANES, row:row + m] = v.T
    s = s_ref[:, 0, :]
    r = s.shape[0]
    m = s * (1.0 / n) - jnp.sum(s, axis=0, keepdims=True) * (1.0 / total)
    mh, ml = split(m)
    mean[:r] = mh
    mean[r:] = ml
    mean_t[...] = jnp.concatenate([mh.astype(F32), ml.astype(F32), mh.astype(F32)], axis=0).T.astype(BF16)
    basis[...] = jnp.concatenate([b_ref[0], b_ref[1]], axis=1)
    cut = d // 2

    @pl.loop(0, ITERS)
    def _(_):
        bf = basis[...]
        inner = dot(mean[...], bf, 1, 0)
        ih, il = split((inner[:r] + inner[r:]) * float(n))
        side = jnp.concatenate([ih, ih, il], axis=0)
        parts = []
        for g in range(2):
            at = slice(g * cut, (g + 1) * cut)
            parts.append(split(dot(w[at, :], bf, 1, 0) + dot(mean_t[at, :], side, 1, 0)))
        hh, cross, ll = 0.0, 0.0, 0.0
        for ph, plo in parts:
            hh += dot(ph, ph, 0, 0)
            cross += dot(plo, ph, 0, 0)
            ll += dot(plo, plo, 0, 0)
        a[...] = hh + (ll + (cross + cross.T))
        inverse_factor(a, spread, k, 64)
        below = lax.broadcasted_iota(jnp.int32, (k, k), 0) >= lax.broadcasted_iota(jnp.int32, (k, k), 1)
        lh, ll = split(jnp.where(below, a[...], 0.0))
        for g, (ph, plo) in enumerate(parts):
            new = dot(ph, lh, 1, 1) + (dot(ph, ll, 1, 1) + dot(plo, lh, 1, 1))
            at = slice(g * cut, (g + 1) * cut)
            half[at, :] = jnp.where(core == 0, new[:, :h], new[:, h:])
            basis[at, :] = new.astype(BF16)

    half_copy = pltpu.make_async_copy(half, basis_hbm, h_sem)
    half_copy.start()

    def out_copy(i):
        at = pl.ds(pl.multiple_of(i * rows, rows), rows)
        return pltpu.make_async_copy(out.at[at], o_hbm.at[at], o_sem.at[i])

    @pl.loop(0, TILES)
    def _(i):
        unit_copy(i).wait()
        for g in range(2):
            at = pl.ds(pl.multiple_of(i * rows + g * (rows // 2), rows // 2), rows // 2)
            coords = dot(unit[at, :], basis[...], 1, 0)
            scale = lax.rsqrt(jnp.sum(coords * coords, axis=1, keepdims=True) * (1.0 / k) + 0.0001)
            out[at, :] = (jnp.where(core == 0, coords[:, :h], coords[:, h:]) * scale).astype(BF16)
        out_copy(i).start()

    half_copy.wait()
    for i in range(TILES):
        out_copy(i).wait()


def finish(n, total, w, s, b, u):
    d, h = b.shape[1], b.shape[2]
    k = 2 * h
    vm = pl.BlockSpec(memory_space=pltpu.VMEM)
    hbm = pl.BlockSpec(memory_space=pl.ANY)
    dma = pltpu.SemaphoreType.DMA
    return pl.pallas_call(
        functools.partial(finish_kernel, n, total),
        in_specs=[vm] * 3 + [hbm],
        out_specs=[hbm] * 2,
        out_shape=[jax.ShapeDtypeStruct((n, h), BF16), jax.ShapeDtypeStruct((d, h), F32)],
        scratch_shapes=[
            pltpu.VMEM((d, d), BF16),
            pltpu.VMEM((d, k), BF16),
            pltpu.VMEM((2 * s.shape[0], d), BF16),
            pltpu.VMEM((d, 3 * s.shape[0]), BF16),
            pltpu.VMEM((k, k), F32),
            pltpu.VMEM((18, 8, LANES), F32),
            pltpu.VMEM((n, d), BF16),
            pltpu.VMEM((n, h), BF16),
            pltpu.VMEM((d, h), F32),
            dma((TILES,)),
            dma((TILES,)),
            dma(()),
        ],
    )(w, s, b, u)


def factors(r):
    z = 4 if r % 4 == 0 else 1
    x = 1
    while x * x < r // z:
        x *= 2
    return z, r // z // x, x


def split3(v):
    hi, rest = split(v)
    rest = v - hi.astype(F32)
    mid = rest.astype(BF16).astype(F32)
    return hi.astype(F32), mid, (rest - mid).astype(BF16).astype(F32)


def stack(parts, order):
    pad = jnp.zeros((16 - len(order), parts[0].shape[1]), F32)
    return jnp.concatenate([parts[i] for i in order] + [pad], axis=0).astype(BF16)


OWNER = (0, 1, 0, 1, 1, 1)
SLOTS = (
    (((0, 0, 3),), ((0, 3, 6),), ((2, 2, 4),), ((2, 4, 6),)),
    (((1, 1, 4),), ((1, 4, 6),), ((3, 3, 6),), ((4, 4, 6), (5, 5, 6))),
)
LAG = 3
UNITS = 12
STEP = 128


def packing(d):
    t = d // len(OWNER)
    firsts, fill = {}, [0, 0]
    for i, c in enumerate(OWNER):
        for l in range(i * t // LANES, d // LANES):
            m = min(t, (l + 1) * LANES - i * t)
            firsts[i, l] = (c, fill[c], m)
            fill[c] += m
    return firsts, fill


def packed_length(d, r):
    unit = 5 * 16 * r
    return -(-max(packing(d)[1]) // unit) * unit


def stream_count(length, r):
    return 10 if length % (160 * r) == 0 else 5


def plans_of(streams):
    return [(("x", "y", "z"), ("y", "x", "z"))[q % 2] for q in range(streams)]


def reduce_kernel(r, e_hbm, b_ref, wout, sout, bout, u_hbm, e, acc, ssum, left, right, w_ref, e_sem, *scratch):
    nz, ny, nx = factors(r)
    n, d = e.shape
    t = d // len(OWNER)
    firsts, fill = packing(d)
    length = w_ref.shape[0]
    streams = stream_count(length, r)
    plans = plans_of(streams)
    size = {"x": nx, "y": ny, "z": nz}
    stride = {"x": 1, "y": nx, "z": nx * ny}
    scratch = list(scratch)
    stage = [[scratch.pop(0) for _ in plan] for plan in plans]
    held = [[scratch.pop(0) for _ in plan[:-1]] for plan in plans]
    w_recv, s_recv, w_send, s_send, c_send, c_recv, b_send, b_recv, u_sem = scratch

    me = lax.axis_index("rows")
    core = lax.axis_index("cols")
    tile = n // TILES

    def tile_copy(i):
        at_rows = pl.ds(pl.multiple_of(i * tile, tile), tile)
        return pltpu.make_async_copy(e_hbm.at[at_rows], e.at[at_rows], e_sem.at[i])

    for i in range(TILES):
        tile_copy(i).start()
    at = {a: lax.rem(me // stride[a], size[a]) for a in size}
    partner = {"cols": 1 - core}

    def peer(a, k):
        p = lax.rem(at[a] + k, size[a])
        return p, {"rows": me + (p - at[a]) * stride[a]}

    barrier = pltpu.get_barrier_semaphore()
    count = 1
    pl.semaphore_signal(barrier, inc=1, device_id=partner, device_id_type=MESH)
    for a in size:
        for k in range(1, size[a]):
            pl.semaphore_signal(barrier, inc=1, device_id=peer(a, k)[1], device_id_type=MESH)
            count += 1
    pl.semaphore_wait(barrier, count)

    def remote(src, dst, send, recv, device):
        pltpu.make_async_remote_copy(
            src_ref=src, dst_ref=dst, send_sem=send, recv_sem=recv, device_id=device, device_id_type=MESH
        ).start()

    def settle(ref, sem):
        pltpu.make_async_copy(ref, ref, sem).wait()

    def rows_of(off, m):
        return pl.ds(pl.multiple_of(off, 16), m)

    off = [q * (length // streams) for q in range(streams)]
    span = [length // streams] * streams

    def start_reduce(q, ph):
        a = plans[q][ph]
        m = span[q] // size[a]
        for k in range(1, size[a]):
            p, dev = peer(a, k)
            src = w_ref.at[rows_of(off[q] + p * m, m)] if ph == 0 else held[q][ph - 1].at[rows_of(p * m, m)]
            remote(src, stage[q][ph].at[k - 1], w_send, w_recv.at[q, ph], dev)

    def finish_reduce(q, ph):
        a = plans[q][ph]
        g = size[a]
        m = span[q] // g
        if g > 1:
            settle(stage[q][ph], w_recv.at[q, ph])
        mine = rows_of(off[q] + at[a] * m, m) if ph == 0 else rows_of(at[a] * m, m)
        total = (w_ref[mine] if ph == 0 else held[q][ph - 1][mine]).astype(F32)
        for k in range(g - 1):
            total = total + stage[q][ph][k].astype(F32)
        off[q] = off[q] + at[a] * m
        span[q] = m
        if ph < len(plans[q]) - 1:
            held[q][ph][...] = total.astype(BF16)
        else:
            wout[core, rows_of(off[q], m)] = total.astype(BF16)

    def start_gather(q, ph):
        a = plans[q][ph]
        block = wout.at[core, rows_of(off[q], span[q])]
        for k in range(1, size[a]):
            remote(block, block, w_send, w_recv.at[q, 3 + ph], peer(a, k)[1])

    def send_across(row, m):
        block = wout.at[core, rows_of(row, m)]
        remote(block, block, c_send, c_recv, partner)

    def finish_gather(q, ph):
        a = plans[q][ph]
        if size[a] > 1:
            settle(stage[q][ph], w_recv.at[q, 3 + ph])
        off[q] = off[q] - at[a] * span[q]
        span[q] = span[q] * size[a]
        if ph == 1:
            send_across(off[q], span[q])
        if ph == 0:
            part = span[q] // size[a]
            for k in range(1, size[a]):
                send_across(off[q] + peer(a, k)[0] * part, part)

    def advance(q, st):
        if st < 3:
            finish_reduce(q, st)
            if st < 2:
                start_reduce(q, st + 1)
            else:
                start_gather(q, 2)
        else:
            finish_gather(q, 5 - st)
            if st < 5:
                start_gather(q, 4 - st)

    def start_sums(ph):
        a = "xyz"[ph]
        width = stride[a]
        block = pl.ds(me // width * width, width)
        for k in range(1, size[a]):
            remote(sout.at[block], sout.at[block], s_send, s_recv.at[ph], peer(a, k)[1])

    def finish_sums(ph):
        a = "xyz"[ph]
        if size[a] > 1:
            settle(sout.at[pl.ds(0, (size[a] - 1) * stride[a])], s_recv.at[ph])

    bout[core] = b_ref[...].astype(BF16)
    remote(bout.at[core], bout.at[core], b_send, b_recv, partner)
    ssum[...] = jnp.zeros_like(ssum)
    started = 0
    ready = [0, 0]
    for slot in range(len(SLOTS[0])):
        for c in range(2):
            @pl.when(core == c)
            def _(slot=slot, c=c):
                work, at_col = [], 0
                for i, lo, hi in SLOTS[c][slot]:
                    work.append((i, lo * t, hi * t, at_col))
                    at_col += (hi - lo) * t
                acc[:, :at_col] = jnp.zeros((t, at_col), F32)
                reps = TILES if slot == 0 else 2
                deep = n // reps

                @pl.loop(0, reps)
                def _(step):
                    if slot == 0:
                        tile_copy(step).wait()
                    part = pl.ds(pl.multiple_of(step * deep, deep), deep)
                    if slot == 0:
                        ssum[...] += dot(jnp.ones((8, deep), BF16), e[part, :], 1, 0)
                    for i, lo, hi, col in work:
                        acc[:, col:col + hi - lo] += dot(e[part, i * t:(i + 1) * t], e[part, lo:hi], 0, 0)

                if slot == 0:
                    sums = ssum[0:1, :]
                    left[...] = stack(split3(sums * (1.0 / n)), (0, 0, 1, 1, 0, 2))
                    right[...] = stack(split3(sums), (0, 1, 0, 1, 2, 0))
                for i, lo, hi, col in work:
                    v = acc[:, col:col + hi - lo] - dot(left[:, i * t:(i + 1) * t], right[:, lo:hi], 0, 0)
                    v = v.astype(BF16)
                    for l in range(lo // LANES, hi // LANES):
                        _, first, m = firsts[i, l]
                        w_ref[first:first + m, :] = v[:m, l * LANES - lo:(l + 1) * LANES - lo]
                if slot == len(SLOTS[0]) - 1 and fill[c] < length:
                    w_ref[fill[c]:length, :] = jnp.zeros((length - fill[c], LANES), BF16)

        for c in range(2):
            for i, lo, hi in SLOTS[c][slot]:
                ready[c] = sum(firsts[i, hi * t // LANES - 1][1:])
        until = streams if slot == len(SLOTS[0]) - 1 else min(ready) * streams // length
        for q in range(started, until):
            start_reduce(q, 0)
        started = until
        if slot == 0:
            sout[me] = ssum[0:1, :]
            start_sums(0)
        elif slot < 3:
            finish_sums(slot - 1)
            start_sums(slot)
    finish_sums(2)
    mean = jnp.sum(sout[:, 0, :], axis=0, keepdims=True) * (1.0 / (n * r))

    def make_unit(i):
        @pl.loop(0, n // UNITS // STEP)
        def _(step):
            at_rows = pl.ds(pl.multiple_of(i * (n // UNITS) + step * STEP, STEP), STEP)
            centered = e[at_rows, :].astype(F32) - mean
            e[at_rows, :] = (
                centered * lax.rsqrt(jnp.sum(centered * centered, axis=1, keepdims=True) + 1.0)
            ).astype(BF16)

        at_rows = pl.ds(i * (n // UNITS), n // UNITS)
        pltpu.make_async_copy(e.at[at_rows], u_hbm.at[at_rows], u_sem).start()

    events = sorted((q + LAG * st, st, q) for q in range(streams) for st in range(6))
    units = 0
    for at_event, (_, st, q) in enumerate(events):
        advance(q, st)
        if at_event % 4 == 1 and units < UNITS:
            make_unit(units)
            units += 1
    while units < UNITS:
        make_unit(units)
        units += 1
    settle(wout.at[0], c_recv)
    settle(wout.at[0], c_send)
    settle(bout.at[0], b_recv)
    settle(bout.at[0], b_send)
    settle(wout.at[:, pl.ds(0, length - length // r)], w_send)
    settle(sout.at[pl.ds(0, r - 1)], s_send)
    pltpu.make_async_copy(e, u_hbm, u_sem).wait()


def reduce(r, e, b):
    n, d = e.shape
    t = d // len(OWNER)
    length = packed_length(d, r)
    nz, ny, nx = factors(r)
    size = {"x": nx, "y": ny, "z": nz}
    streams = stream_count(length, r)
    stages, helds = [], []
    for plan in plans_of(streams):
        m = length // streams
        for ph, a in enumerate(plan):
            m //= size[a]
            stages.append(pltpu.VMEM((max(size[a] - 1, 1), m, LANES), BF16))
            if ph < 2:
                helds.append(pltpu.VMEM((m, LANES), BF16))
    vm = pl.BlockSpec(memory_space=pltpu.VMEM)
    hbm = pl.BlockSpec(memory_space=pl.ANY)
    dma = pltpu.SemaphoreType.DMA
    return pl.pallas_call(
        functools.partial(reduce_kernel, r),
        in_specs=[hbm, vm],
        out_specs=[vm] * 3 + [hbm],
        out_shape=[
            jax.ShapeDtypeStruct((2, length, LANES), BF16),
            jax.ShapeDtypeStruct((r, 1, d), F32),
            jax.ShapeDtypeStruct((2,) + b.shape, BF16),
            jax.ShapeDtypeStruct((n, d), BF16),
        ],
        scratch_shapes=[
            pltpu.VMEM((n, d), BF16),
            pltpu.VMEM((t, 3 * t), F32),
            pltpu.VMEM((8, d), F32),
            pltpu.VMEM((16, d), BF16),
            pltpu.VMEM((16, d), BF16),
            pltpu.VMEM((length, LANES), BF16),
            dma((TILES,)),
        ]
        + stages + helds + [dma((streams, 6)), dma((3,))] + [dma(())] * 7,
        compiler_params=pltpu.CompilerParams(collective_id=0, has_side_effects=True),
    )(e, b)


def shards(embeddings, start_basis):
    n, d = embeddings.shape
    r = lax.axis_size("rows")
    w, s, b, u = reduce(r, embeddings, start_basis)
    return finish(n, n * r, w, s, b, u)


def solution(mesh):
    in_specs = (P("rows", None), P(None, "cols"))
    out_specs = (P("rows", "cols"), P(None, "cols"))
    return jax.shard_map(shards, mesh=mesh, in_specs=in_specs, out_specs=out_specs, check_vma=False)
```

time: 127 us -> 93.4 us (0.74)
  Pallas kernels: 124 us -> 92.4 us
  other arithmetic: 1.92 us -> 0 us
    pallas_call x3 -> x2, Pallas kernels: 124 us -> 92.4 us  [the longest x1 51.3 us: reduce(): pl.pallas_call(functools.partial(reduce_kernel, r), in_specs=[hbm, vm], o...]
    convert_element_type x1 -> x0, other arithmetic: 1.92 us -> none  [shards(): start_basis.astype(BF16)]
where the time goes in v1:
time: 93.4 us; the launch traced here: 93.2 us
  Pallas kernels  92.4 us (99%)
    pallas_call x1, Pallas kernels, reduce(): pl.pallas_call(functools.partial(reduce_kernel, r), in_specs=[hbm, vm], o...  51.3 us
    pallas_call x1, Pallas kernels, finish(): pl.pallas_call(functools.partial(finish_kernel, n, total), in_specs=[vm]...  41.1 us

profile of v1, /device:TPU:0, one launch (start us, length us, event | category | flops | bytes accessed | tf_op | source)
XLA Modules:
  0.0 93.2 jit_solution(15490694892591862133)
XLA Ops:
  0.6 51.3 %shard_map.41 = (bf16[2,5120,128]{2,1,0:T(8,128)(2,1)}, f32[16,1,1536]{2,1,0:T(1,128)}, bf16[2,1536,128]{2,1,0:T(8,128)(2,1)}, bf16[3072,1536]{1,0:T(8,128)(2,1)}) custom-call(bf16[3072,1536]{1,0:T(8,128)(2,1)} %e_hbm.1, f32[1536,128]{1,0:T(8,128)} %b_ref.1), custom_call_target="tpu_custom_call" | custom-call | tf_op jit(solution)/shard_map/pallas_call | solution.py:482
  52.0 41.1 %shard_map.42 = (bf16[3072,128]{1,0:T(8,128)(2,1)}, f32[1536,128]{1,0:T(8,128)}) custom-call(bf16[2,5120,128]{2,1,0:T(8,128)(2,1)} %get-tuple-element.6.w_ref, f32[16,1,1536]{2,1,0:T(1,128)} %get-tuple-element.7.s_ref, bf16[2,1536,128]{2,1,0:T(8,128)(2,1)} %get-tuple-element.8.b_ref, bf16[3072,1536]{1,0:T(8,128)(2,1)} %get-tuple-element.9.u_hbm), custom_call_target="tpu_custom_call" | custom-call | tf_op jit(solution)/shard_map/pallas_call | solution.py:174

commit v2 on v1

--- a/solution.py
+++ b/solution.py
@@ -11,6 +11,7 @@
 LANES = 128
 MESH = pl.DeviceIdType.MESH
 TILES = 4
+VMEM = 32 << 20
 HI = lax.Precision.HIGHEST
 F32 = jnp.float32
 BF16 = jnp.bfloat16
@@ -128,12 +129,19 @@
         for g in range(2):
             at = slice(g * cut, (g + 1) * cut)
             parts.append(split(dot(w[at, :], bf, 1, 0) + dot(mean_t[at, :], side, 1, 0)))
-        hh, cross, ll = 0.0, 0.0, 0.0
-        for ph, plo in parts:
-            hh += dot(ph, ph, 0, 0)
-            cross += dot(plo, ph, 0, 0)
-            ll += dot(plo, plo, 0, 0)
-        a[...] = hh + (ll + (cross + cross.T))
+        for corner in (LANES, k):
+            hh, cross, ll = 0.0, 0.0, 0.0
+            for ph, plo in parts:
+                ph, plo = ph[:, :corner], plo[:, :corner]
+                hh += dot(ph, ph, 0, 0)
+                cross += dot(plo, ph, 0, 0)
+                ll += dot(plo, plo, 0, 0)
+            part = hh + (ll + (cross + cross.T))
+            if corner < k:
+                a[:corner, :corner] = part
+            else:
+                a[:LANES, LANES:] = part[:LANES, LANES:]
+                a[LANES:, :] = part[LANES:, :]
         inverse_factor(a, spread, k, 64)
         below = lax.broadcasted_iota(jnp.int32, (k, k), 0) >= lax.broadcasted_iota(jnp.int32, (k, k), 1)
         lh, ll = split(jnp.where(below, a[...], 0.0))
@@ -169,7 +177,7 @@
     d, h = b.shape[1], b.shape[2]
     k = 2 * h
     vm = pl.BlockSpec(memory_space=pltpu.VMEM)
-    hbm = pl.BlockSpec(memory_space=pl.ANY)
+    hbm = pl.BlockSpec(memory_space=pltpu.HBM)
     dma = pltpu.SemaphoreType.DMA
     return pl.pallas_call(
         functools.partial(finish_kernel, n, total),
@@ -190,6 +198,7 @@
             dma((TILES,)),
             dma(()),
         ],
+        compiler_params=pltpu.CompilerParams(vmem_limit_bytes=VMEM),
     )(w, s, b, u)
 
 
@@ -218,7 +227,6 @@
     (((0, 0, 3),), ((0, 3, 6),), ((2, 2, 4),), ((2, 4, 6),)),
     (((1, 1, 4),), ((1, 4, 6),), ((3, 3, 6),), ((4, 4, 6), (5, 5, 6))),
 )
-LAG = 3
 UNITS = 12
 STEP = 128
 
@@ -243,8 +251,63 @@
     return 10 if length % (160 * r) == 0 else 5
 
 
+PLANS = ("xyz", "yxz", "xyz", "yxz", "zxy")
+SLOT_US = (3.3, 1.2, 1.2, 1.4)
+RATE = 87e3
+FLIGHT_US = {"x": 2.2, "y": 2.2, "z": 2.9}
+STEP_US = 0.2
+UNIT_US = 0.5
+
+
 def plans_of(streams):
-    return [(("x", "y", "z"), ("y", "x", "z"))[q % 2] for q in range(streams)]
+    return [PLANS[q % len(PLANS)] for q in range(streams)]
+
+
+def timetable(streams, plans, size, chunk, until):
+    free = dict.fromkeys("xyz", 0.0)
+    due, table = {}, []
+    now, left = 0.0, UNITS
+
+    def launch(q, st):
+        plan = plans[q]
+        ph = min(st, 5 - st)
+        share = chunk
+        for a in plan[:ph + 1]:
+            share /= size[a]
+        g = size[plan[ph]]
+        free[plan[ph]] = max(now, free[plan[ph]]) + share * (g // 2) * (g - g // 2) / RATE
+        due[q] = (free[plan[ph]] + FLIGHT_US[plan[ph]], q, st)
+
+    def take(at):
+        _, q, st = at
+        del due[q]
+        if st < 5:
+            launch(q, st + 1)
+        return st, q
+
+    started = 0
+    for cost, stop in zip(SLOT_US, until):
+        now += cost
+        for q in range(started, stop):
+            launch(q, 0)
+        started = stop
+        step = []
+        if stop < streams:
+            for at in sorted(v for v in due.values() if v[0] <= now):
+                now += STEP_US
+                step.append(take(at))
+        table.append(step)
+    while due:
+        at = min(due.values())
+        if left and at[0] - now > 0.3:
+            now += UNIT_US
+            left -= 1
+            table[-1].append(None)
+        else:
+            now = max(now, at[0]) + STEP_US
+            table[-1].append(take(at))
+    table[-1] += [None] * left
+    return table
 
 
 def reduce_kernel(r, e_hbm, b_ref, wout, sout, bout, u_hbm, e, acc, ssum, left, right, w_ref, e_sem, *scratch):
@@ -377,8 +440,13 @@
     bout[core] = b_ref[...].astype(BF16)
     remote(bout.at[core], bout.at[core], b_send, b_recv, partner)
     ssum[...] = jnp.zeros_like(ssum)
+    until = []
+    for slots in zip(*SLOTS):
+        ends = [sum(firsts[work[-1][0], work[-1][2] * t // LANES - 1][1:]) for work in slots]
+        until.append(min(ends) * streams // length)
+    until[-1] = streams
+    table = timetable(streams, plans, size, 4 * LANES * length // streams, until)
     started = 0
-    ready = [0, 0]
     for slot in range(len(SLOTS[0])):
         for c in range(2):
             @pl.when(core == c)
@@ -414,13 +482,12 @@
                 if slot == len(SLOTS[0]) - 1 and fill[c] < length:
                     w_ref[fill[c]:length, :] = jnp.zeros((length - fill[c], LANES), BF16)
 
-        for c in range(2):
-            for i, lo, hi in SLOTS[c][slot]:
-                ready[c] = sum(firsts[i, hi * t // LANES - 1][1:])
-        until = streams if slot == len(SLOTS[0]) - 1 else min(ready) * streams // length
-        for q in range(started, until):
+        for q in range(started, until[slot]):
             start_reduce(q, 0)
-        started = until
+        started = until[slot]
+        if slot < len(SLOTS[0]) - 1:
+            for st, q in table[slot]:
+                advance(q, st)
         if slot == 0:
             sout[me] = ssum[0:1, :]
             start_sums(0)
@@ -442,16 +509,13 @@
         at_rows = pl.ds(i * (n // UNITS), n // UNITS)
         pltpu.make_async_copy(e.at[at_rows], u_hbm.at[at_rows], u_sem).start()
 
-    events = sorted((q + LAG * st, st, q) for q in range(streams) for st in range(6))
     units = 0
-    for at_event, (_, st, q) in enumerate(events):
-        advance(q, st)
-        if at_event % 4 == 1 and units < UNITS:
+    for event in table[-1]:
+        if event is None:
             make_unit(units)
             units += 1
-    while units < UNITS:
-        make_unit(units)
-        units += 1
+        else:
+            advance(event[1], event[0])
     settle(wout.at[0], c_recv)
     settle(wout.at[0], c_send)
     settle(bout.at[0], b_recv)
@@ -477,7 +541,7 @@
             if ph < 2:
                 helds.append(pltpu.VMEM((m, LANES), BF16))
     vm = pl.BlockSpec(memory_space=pltpu.VMEM)
-    hbm = pl.BlockSpec(memory_space=pl.ANY)
+    hbm = pl.BlockSpec(memory_space=pltpu.HBM)
     dma = pltpu.SemaphoreType.DMA
     return pl.pallas_call(
         functools.partial(reduce_kernel, r),
@@ -499,7 +563,7 @@
             dma((TILES,)),
         ]
         + stages + helds + [dma((streams, 6)), dma((3,))] + [dma(())] * 7,
-        compiler_params=pltpu.CompilerParams(collective_id=0, has_side_effects=True),
+        compiler_params=pltpu.CompilerParams(collective_id=0, has_side_effects=True, vmem_limit_bytes=VMEM),
     )(e, b)
 
 

time: 93.4 us -> 88.7 us (0.950)
  Pallas kernels: 92.4 us -> 86.6 us
  local copies, waits for them, and re-layouts: 0 us -> 1.13 us
    pallas_call x1, Pallas kernels: 51.3 us -> 47.7 us  [reduce(): pl.pallas_call(functools.partial(reduce_kernel, r), in_specs=[hbm, vm], o...]
    pallas_call x1, Pallas kernels: 41.1 us -> 39 us  [finish(): pl.pallas_call(functools.partial(finish_kernel, n, total), in_specs=[vm]...]
    unnamed x0 -> x2, local copies, waits for them, and re-layouts: none -> 1.13 us
where the time goes in v2:
time: 88.7 us; the launch traced here: 88.6 us
  Pallas kernels  86.6 us (98%)
  local copies, waits for them, and re-layouts  1.13 us (1%)
    pallas_call x1, Pallas kernels, reduce(): pl.pallas_call(functools.partial(reduce_kernel, r), in_specs=[hbm, vm], o...  47.7 us
    pallas_call x1, Pallas kernels, finish(): pl.pallas_call(functools.partial(finish_kernel, n, total), in_specs=[vm]...  39 us

profile of v2, /device:TPU:0, one launch (start us, length us, event | category | flops | bytes accessed | tf_op | source)
XLA Modules:
  0.0 88.6 jit_solution(7053356798392408830)
XLA Ops:
  0.6 0.0 copy-start
  0.6 1.1 %copy-done = f32[1536,128]{1,0:T(8,128)S(1)} copy-done((f32[1536,128]{1,0:T(8,128)S(1)}, f32[1536,128]{1,0:T(8,128)}, u32[]{:S(2)}) %copy-start) | copy-done | bytes 786456
  1.8 47.7 %shard_map.41 = (bf16[2,5120,128]{2,1,0:T(8,128)(2,1)S(1)}, f32[16,1,1536]{2,1,0:T(1,128)S(1)}, bf16[2,1536,128]{2,1,0:T(8,128)(2,1)S(1)}, bf16[3072,1536]{1,0:T(8,128)(2,1)S(1)}) custom-call(bf16[3072,1536]{1,0:T(8,128)(2,1)} %e_hbm.1, f32[1536,128]{1,0:T(8,128)S(1)} %copy-done), custom_call_target="tpu_custom_call" | custom-call | tf_op jit(solution)/shard_map/pallas_call | solution.py:546
  49.5 39.0 %shard_map.42 = (bf16[3072,128]{1,0:T(8,128)(2,1)}, f32[1536,128]{1,0:T(8,128)}) custom-call(bf16[2,5120,128]{2,1,0:T(8,128)(2,1)S(1)} %get-tuple-element.6.w_ref, f32[16,1,1536]{2,1,0:T(1,128)S(1)} %get-tuple-element.7.s_ref, bf16[2,1536,128]{2,1,0:T(8,128)(2,1)S(1)} %get-tuple-element.8.b_ref, bf16[3072,1536]{1,0:T(8,128)(2,1)S(1)} %get-tuple-element.9.u_hbm), custom_call_target="tpu_custom_call" | custom-call | tf_op jit(solution)/shard_map/pallas_call | solution.py:182
Async XLA Ops:
  0.6 1.1 %copy-start = (f32[1536,128]{1,0:T(8,128)S(1)}, f32[1536,128]{1,0:T(8,128)}, u32[]{:S(2)}) copy-start(f32[1536,128]{1,0:T(8,128)} %b_ref.1) | copy-start | bytes 2359300

commit v3 on v2

--- a/solution.py
+++ b/solution.py
@@ -11,6 +11,7 @@
 LANES = 128
 MESH = pl.DeviceIdType.MESH
 TILES = 4
+NEAR = 1
 VMEM = 32 << 20
 HI = lax.Precision.HIGHEST
 F32 = jnp.float32
@@ -26,65 +27,72 @@
     return hi, (v - hi.astype(F32)).astype(BF16)
 
 
-def inverse_factor(a_ref, spread, k, b):
-    w = 2 * b
-    lanes = lax.broadcasted_iota(jnp.int32, (b, w), 1)
-    subs = lax.broadcasted_iota(jnp.int32, (b, w), 0)
+def inverse_factor(a_ref, spread, k):
+    b = LANES
+    m = b // 8
+    sub = lax.broadcasted_iota(jnp.int32, (8, b), 0)
+    lane = lax.broadcasted_iota(jnp.int32, (8, b), 1)
     wide_lane = lax.broadcasted_iota(jnp.int32, (b, k), 1)
     wide_sub = lax.broadcasted_iota(jnp.int32, (b, k), 0)
-    sub = lax.broadcasted_iota(jnp.int32, (8, w), 0)
-    m = b // 8
-    for blk in range(k // b):
-        lo, hi = blk * b, (blk + 1) * b
-        base = lo % w
-        other = b - base
-        here = (lanes >= base) & (lanes < base + b)
-        first = lo - base
-        aug = jnp.where(here, a_ref[lo:hi, first:first + w], (lanes - other == subs).astype(F32))
-        tiles = [aug[8 * t:8 * t + 8] for t in range(m)]
+    for lo in range(0, k, b):
+        hi = lo + b
+        left = [a_ref[lo + 8 * t:lo + 8 * t + 8, lo:hi] for t in range(m)]
+        right = [(lane == sub + 8 * t).astype(F32) for t in range(m)]
         for p in range(m):
             cols = {
-                t: [jnp.broadcast_to(tiles[t][:, base + 8 * p + c:base + 8 * p + c + 1], (8, w)) for c in range(8)]
+                t: [jnp.broadcast_to(left[t][:, 8 * p + c:8 * p + c + 1], (8, b)) for c in range(8)]
                 for t in range(p, m)
             }
-            slot = 9 * (p % 2)
+            slot = 10 * (p % 2)
             for j in range(8):
                 spread[slot + j] = cols[p][j]
-            spread[slot + 8] = tiles[p]
-            a = [[jnp.broadcast_to(spread[slot + j, i:i + 1, :], (8, w)) for j in range(i + 1)] for i in range(8)]
-            low = [jnp.broadcast_to(spread[slot + 8, c:c + 1, :], (8, w)) for c in range(8)]
-            inv = []
+            spread[slot + 8] = left[p]
+            spread[slot + 9] = right[p]
+            a = [[jnp.broadcast_to(spread[slot + j, i:i + 1, :], (8, b)) for j in range(i + 1)] for i in range(8)]
+            low = [[jnp.broadcast_to(spread[slot + 8 + h, c:c + 1, :], (8, b)) for c in range(8)] for h in range(2)]
+            close = range(p + 1, min(p + 1 + NEAR, m))
+            inv, f = [], [[None] * 8 for _ in range(8)]
             for j in range(8):
                 r = 1.0 / a[j][j]
                 inv.append(r)
-                f = {i: a[i][j] * r for i in range(j + 1, 8)}
                 for i in range(j + 1, 8):
+                    f[i][j] = a[i][j] * r
                     for c in range(j + 1, i + 1):
-                        a[i][c] = a[i][c] - f[i] * a[c][j]
-                scaled = low[j] * r
-                for i in range(j + 1, 8):
-                    low[i] = low[i] - f[i] * low[j]
-                for t in range(p + 1, m):
-                    tiles[t] = tiles[t] - cols[t][j] * scaled
+                        a[i][c] = a[i][c] - f[i][j] * a[c][j]
+                for h in range(2):
                     for i in range(j + 1, 8):
-                        cols[t][i] = cols[t][i] - f[i] * cols[t][j]
-            v, d = low[0], inv[0]
+                        low[h][i] = low[h][i] - f[i][j] * low[h][j]
+                for t in close:
+                    z = cols[t][j] * r
+                    left[t] = left[t] - z * low[0][j]
+                    right[t] = right[t] - z * low[1][j]
+                    for i in range(j + 1, 8):
+                        cols[t][i] = cols[t][i] - f[i][j] * cols[t][j]
+            if p + 1 + NEAR < m:
+                solved = [[low[h][i] * inv[i] for i in range(8)] for h in range(2)]
+                for h in range(2):
+                    for i in range(6, -1, -1):
+                        v = solved[h][i]
+                        for c in range(7, i, -1):
+                            v = v - f[c][i] * solved[h][c]
+                        solved[h][i] = v
+                for t in range(p + 1 + NEAR, m):
+                    for h, part in enumerate((left, right)):
+                        u = [cols[t][c] * solved[h][c] for c in range(8)]
+                        part[t] = part[t] - (((u[7] + u[6]) + (u[5] + u[4])) + ((u[3] + u[2]) + (u[1] + u[0])))
+            v, d = low[1][0], inv[0]
             for i in range(1, 8):
-                v = jnp.where(sub == i, low[i], v)
+                v = jnp.where(sub == i, low[1][i], v)
                 d = jnp.where(sub == i, inv[i], d)
             root = lax.rsqrt(d)
             root = root * (1.5 - 0.5 * d * root * root)
-            tiles[p] = v * (d * root)
-        factor = jnp.where(here, 0.0, jnp.concatenate(tiles, axis=0))
+            right[p] = v * (d * root)
+        factor = jnp.concatenate(right, axis=0)
         inside = (wide_lane >= lo) & (wide_lane < hi)
-        rows = jnp.where(inside, (wide_lane - lo == wide_sub).astype(F32), a_ref[lo:hi, :])
-        pad = jnp.zeros((b, k), F32)
-        strip = dot(factor, jnp.concatenate([pad, rows] if base == 0 else [rows, pad], axis=0), 1, 0, HI)
+        strip = dot(factor, jnp.where(inside, (wide_lane - lo == wide_sub).astype(F32), a_ref[lo:hi, :]), 1, 0, HI)
         for r0 in range(hi, k, b):
-            turned = pltpu.roll(a_ref[r0:r0 + b, first:first + w], b, axis=1)
-            left = dot(turned, factor, 1, 1, HI)
-            old = jnp.where(inside, 0.0, a_ref[r0:r0 + b, :])
-            a_ref[r0:r0 + b, :] = old - dot(left, strip, 1, 0, HI)
+            turned = dot(a_ref[r0:r0 + b, lo:hi], factor, 1, 1, HI)
+            a_ref[r0:r0 + b, :] = jnp.where(inside, 0.0, a_ref[r0:r0 + b, :]) - dot(turned, strip, 1, 0, HI)
         a_ref[lo:hi, :] = strip
 
 
@@ -142,7 +150,7 @@
             else:
                 a[:LANES, LANES:] = part[:LANES, LANES:]
                 a[LANES:, :] = part[LANES:, :]
-        inverse_factor(a, spread, k, 64)
+        inverse_factor(a, spread, k)
         below = lax.broadcasted_iota(jnp.int32, (k, k), 0) >= lax.broadcasted_iota(jnp.int32, (k, k), 1)
         lh, ll = split(jnp.where(below, a[...], 0.0))
         for g, (ph, plo) in enumerate(parts):
@@ -190,7 +198,7 @@
             pltpu.VMEM((2 * s.shape[0], d), BF16),
             pltpu.VMEM((d, 3 * s.shape[0]), BF16),
             pltpu.VMEM((k, k), F32),
-            pltpu.VMEM((18, 8, LANES), F32),
+            pltpu.VMEM((20, 8, LANES), F32),
             pltpu.VMEM((n, d), BF16),
             pltpu.VMEM((n, h), BF16),
             pltpu.VMEM((d, h), F32),
@@ -254,9 +262,10 @@
 PLANS = ("xyz", "yxz", "xyz", "yxz", "zxy")
 SLOT_US = (3.3, 1.2, 1.2, 1.4)
 RATE = 87e3
-FLIGHT_US = {"x": 2.2, "y": 2.2, "z": 2.9}
+FLIGHT_US = {"x": 3.0, "y": 3.0, "z": 4.0}
 STEP_US = 0.2
 UNIT_US = 0.5
+SUM_EVENTS = (0, 5, 10)
 
 
 def plans_of(streams):
@@ -299,7 +308,7 @@
         table.append(step)
     while due:
         at = min(due.values())
-        if left and at[0] - now > 0.3:
+        if left and at[0] - now > 0.3 and len(table[-1]) > SUM_EVENTS[-1]:
             now += UNIT_US
             left -= 1
             table[-1].append(None)
@@ -491,13 +500,8 @@
         if slot == 0:
             sout[me] = ssum[0:1, :]
             start_sums(0)
-        elif slot < 3:
-            finish_sums(slot - 1)
-            start_sums(slot)
-    finish_sums(2)
-    mean = jnp.sum(sout[:, 0, :], axis=0, keepdims=True) * (1.0 / (n * r))
-
-    def make_unit(i):
+
+    def make_unit(i, mean):
         @pl.loop(0, n // UNITS // STEP)
         def _(step):
             at_rows = pl.ds(pl.multiple_of(i * (n // UNITS) + step * STEP, STEP), STEP)
@@ -509,13 +513,22 @@
         at_rows = pl.ds(i * (n // UNITS), n // UNITS)
         pltpu.make_async_copy(e.at[at_rows], u_hbm.at[at_rows], u_sem).start()
 
-    units = 0
+    units, count = 0, 0
     for event in table[-1]:
         if event is None:
-            make_unit(units)
+            make_unit(units, mean)
             units += 1
-        else:
-            advance(event[1], event[0])
+            continue
+        if count in SUM_EVENTS:
+            ph = SUM_EVENTS.index(count)
+            finish_sums(ph)
+            if ph < 2:
+                start_sums(ph + 1)
+            else:
+                fresh = jnp.sum(sout[:, 0, :], axis=0, keepdims=True)
+                mean = fresh * (1.0 / (n * r))
+        count += 1
+        advance(event[1], event[0])
     settle(wout.at[0], c_recv)
     settle(wout.at[0], c_send)
     settle(bout.at[0], b_recv)

time: 88.7 us -> 85 us (0.958)
  Pallas kernels: 86.6 us -> 82.9 us
    pallas_call x1, Pallas kernels: 47.7 us -> 44.7 us  [reduce(): pl.pallas_call(functools.partial(reduce_kernel, r), in_specs=[hbm, vm], o...]
where the time goes in v3:
time: 85 us; the launch traced here: 84.8 us
  Pallas kernels  82.9 us (98%)
  local copies, waits for them, and re-layouts  1.13 us (1%)
    pallas_call x1, Pallas kernels, reduce(): pl.pallas_call(functools.partial(reduce_kernel, r), in_specs=[hbm, vm], o...  44.7 us
    pallas_call x1, Pallas kernels, finish(): pl.pallas_call(functools.partial(finish_kernel, n, total), in_specs=[vm]...  38.2 us

profile of v3, /device:TPU:0, one launch (start us, length us, event | category | flops | bytes accessed | tf_op | source)
XLA Modules:
  0.0 84.8 jit_solution(12099639982021981190)
XLA Ops:
  0.6 0.0 copy-start
  0.6 1.1 %copy-done = f32[1536,128]{1,0:T(8,128)S(1)} copy-done((f32[1536,128]{1,0:T(8,128)S(1)}, f32[1536,128]{1,0:T(8,128)}, u32[]{:S(2)}) %copy-start) | copy-done | bytes 786456
  1.8 44.7 %shard_map.41 = (bf16[2,5120,128]{2,1,0:T(8,128)(2,1)S(1)}, f32[16,1,1536]{2,1,0:T(1,128)S(1)}, bf16[2,1536,128]{2,1,0:T(8,128)(2,1)S(1)}, bf16[3072,1536]{1,0:T(8,128)(2,1)S(1)}) custom-call(bf16[3072,1536]{1,0:T(8,128)(2,1)} %e_hbm.1, f32[1536,128]{1,0:T(8,128)S(1)} %copy-done), custom_call_target="tpu_custom_call" | custom-call | tf_op jit(solution)/shard_map/pallas_call | solution.py:559
  46.5 38.2 %shard_map.42 = (bf16[3072,128]{1,0:T(8,128)(2,1)}, f32[1536,128]{1,0:T(8,128)}) custom-call(bf16[2,5120,128]{2,1,0:T(8,128)(2,1)S(1)} %get-tuple-element.6.w_ref, f32[16,1,1536]{2,1,0:T(1,128)S(1)} %get-tuple-element.7.s_ref, bf16[2,1536,128]{2,1,0:T(8,128)(2,1)S(1)} %get-tuple-element.8.b_ref, bf16[3072,1536]{1,0:T(8,128)(2,1)S(1)} %get-tuple-element.9.u_hbm), custom_call_target="tpu_custom_call" | custom-call | tf_op jit(solution)/shard_map/pallas_call | solution.py:190
Async XLA Ops:
  0.6 1.1 %copy-start = (f32[1536,128]{1,0:T(8,128)S(1)}, f32[1536,128]{1,0:T(8,128)}, u32[]{:S(2)}) copy-start(f32[1536,128]{1,0:T(8,128)} %b_ref.1) | copy-start | bytes 2359300
